TPU v7x, 32 devices: a whole 2x2x4 slice. The times are simulated.
32 devices in a mesh: tm: 32 (over z, y, x, core), prod: 1.
Axes of the slice: x: 2, y: 2, z: 4, core: 2. Of those that a mesh axis runs over, the one named last changes fastest.
Arguments:
- sales_records: float32 [1024, 16, 16, 128], P('tm', 'prod'), may hold values from -6 to 6
- day_month: int32 [1024], replicated, may hold values from 0 to 31, as said below
- month_year: int32 [32], replicated, may hold values from 0 to 3, never falling along the last dimension, each value on 1 to 16 neighbouring positions
- product_category: int32 [16], replicated, may hold values from 0 to 31
- store_region: int32 [16], replicated, may hold values from 0 to 3
Outputs:
- month_detail: float32 [32, 32, 4, 128], P('tm', 'prod')
- month_category: float32 [32, 32, 128], P('tm', 'prod')
- month_region: float32 [32, 4, 128], P('tm')
- month_totals: float32 [32, 128], P('tm')
- year_detail: float32 [4, 32, 4, 128], replicated
- year_category: float32 [4, 32, 128], replicated
- year_region: float32 [4, 4, 128], replicated
- year_totals: float32 [4, 128], replicated
Inputs may be any that keep to these rules, and one draw needn't show every extreme that they name: `day_month`: never falls along the days; month m, for m of 1 to 31, begins at a day from m * 32 - 31 // 2 to m * 32 + 31 // 2, and both ends of that range are taken in every draw. `month_year`: never falls along the months; every year has 1 to 16 months, one exactly that many.
All inputs are finite; a program needn't handle non-finite values.
Results may differ from a plain program's by a relative error of at most 0.0001.
Values sent between devices are 32-bit elements; how exact they have to be, the bound alone decides.
No kernel may reach another device: no remote copies, remote signals or barrier semaphores. Data moves between devices by JAX's collectives and lax.ppermute only.
A program may use at most 64 MiB of HBM per device.

v0:
```python
import jax
import jax.numpy as jnp
from jax import lax
from jax.sharding import PartitionSpec as P

MON_DEV = 1
CATEGORY_COUNT = 32
REGION_COUNT = 4


def with_halo(block, sides, width):
    for axis, dim in sides:
        count = lax.axis_size(axis)
        forward = [(i, i + 1) for i in range(count - 1)]
        backward = [(target, source) for source, target in forward]
        low = lax.ppermute(
            lax.slice_in_dim(block, block.shape[dim] - width, None, axis=dim), axis, forward
        )
        high = lax.ppermute(lax.slice_in_dim(block, 0, width, axis=dim), axis, backward)
        block = jnp.concatenate([low, block, high], axis=dim)
    return block


def onehot(labels, width):
    return (labels[:, None] == jnp.arange(width, dtype=jnp.int32)[None, :]).astype(jnp.float32)


def scaled(sums, counts):
    return sums / jnp.sqrt(counts)


def shards(sales_records, day_month, month_year, product_category, store_region):
    highest = lax.Precision.HIGHEST
    day_dev = sales_records.shape[0]
    prod_dev = sales_records.shape[1]
    stores = float(sales_records.shape[2])
    month_width = month_year.shape[0]
    year_width = max(month_width // 8, 2)
    cats_dev = CATEGORY_COUNT // lax.axis_size("prod")
    products = float(prod_dev * lax.axis_size("prod"))
    time_index = lax.axis_index("tm")
    prod_index = lax.axis_index("prod")
    month_hot = onehot(day_month, month_width)
    year_hot = onehot(month_year, year_width)
    category_hot = onehot(product_category, CATEGORY_COUNT)
    region_hot = onehot(store_region, REGION_COUNT)
    local_products = lax.dynamic_slice_in_dim(category_hot, prod_index * prod_dev, prod_dev, 0)
    by_region = jnp.einsum("dpsq,sr->dprq", sales_records, region_hot, precision=highest)
    by_category = jnp.einsum("dprq,pc->dcrq", by_region, local_products, precision=highest)
    month_days = jnp.sum(month_hot, 0)
    year_days = jnp.dot(month_days, year_hot, precision=highest)
    category_size = jnp.sum(category_hot, 0)
    region_size = jnp.sum(region_hot, 0)
    own_days = lax.dynamic_slice_in_dim(month_days, time_index * MON_DEV, MON_DEV, 0)
    own_sizes = lax.dynamic_slice_in_dim(category_size, prod_index * cats_dev, cats_dev, 0)
    local_labels = lax.dynamic_slice_in_dim(day_month, time_index * day_dev, day_dev, 0)
    window_ids = time_index - 1 + jnp.arange(3, dtype=jnp.int32)
    window_hot = (local_labels[:, None] == window_ids[None, :]).astype(jnp.float32)
    partial_value = jnp.einsum("dcrq,dk->kcrq", by_category, window_hot, precision=highest)
    clipped = jnp.clip(window_ids, 0, month_width - 1)
    inside = ((window_ids >= 0) & (window_ids < month_width)).astype(jnp.float32)
    source_years = onehot(month_year[clipped], year_width) * inside[:, None]
    padded = with_halo(partial_value, (("tm", 0),), 1)
    summed = padded[0:1] + padded[2:3] + padded[4:5]
    detail = lax.psum_scatter(summed, "prod", scatter_dimension=1, tiled=True)
    year_part = jnp.einsum("mcrq,my->ycrq", partial_value, source_years, precision=highest)
    year_cube = lax.psum(year_part, ("tm", "prod"))
    cell = own_days[:, None, None] * own_sizes[None, :, None] * region_size[None, None, :]
    month_detail = scaled(detail, jnp.maximum(cell, 1.0)[..., None])
    month_cat = jnp.sum(detail, 2)
    month_category = scaled(
        month_cat, jnp.maximum(own_days[:, None] * own_sizes[None, :] * stores, 1.0)[..., None]
    )
    month_reg = lax.psum(jnp.sum(detail, 1), "prod")
    month_region = scaled(
        month_reg, jnp.maximum(own_days[:, None] * products * region_size[None, :], 1.0)[..., None]
    )
    month_totals = scaled(jnp.sum(month_reg, 1), (own_days * products * stores)[:, None])
    year_cell = year_days[:, None, None] * category_size[None, :, None] * region_size[None, None, :]
    year_detail = scaled(year_cube, jnp.maximum(year_cell, 1.0)[..., None])
    year_cat = jnp.sum(year_cube, 2)
    year_category = scaled(
        year_cat, jnp.maximum(year_days[:, None] * category_size[None, :] * stores, 1.0)[..., None]
    )
    year_reg = jnp.sum(year_cube, 1)
    year_region = scaled(
        year_reg, jnp.maximum(year_days[:, None] * products * region_size[None, :], 1.0)[..., None]
    )
    year_totals = scaled(jnp.sum(year_reg, 1), (year_days * products * stores)[:, None])
    return (
        month_detail,
        month_category,
        month_region,
        month_totals,
        year_detail,
        year_category,
        year_region,
        year_totals,
    )


def solution(mesh):
    placed = (P("tm", "prod", None, None), P(), P(), P(), P())
    return jax.shard_map(
        shards,
        mesh=mesh,
        in_specs=placed,
        out_specs=(
            P("tm", "prod", None, None),
            P("tm", "prod", None),
            P("tm", None, None),
            P("tm", None),
            P(),
            P(),
            P(),
            P(),
        ),
        check_vma=False,
    )
```

profile of v0, /device:TPU:0, one launch (start us, length us, event | category | flops | bytes accessed | tf_op | source)
XLA Modules:
  0.0 163.1 jit_solution(17972851459997069887)
XLA Ops:
  7.2 3.8 %convolution_bitcast_fusion.1 = f32[32,16,4,128]{3,2,1,0:T(4,128)S(1)} fusion(f32[32,16,16,128]{3,2,1,0:T(8,128)} %param.5, s32[16]{0:T(128)} %param.9), kind=kOutput, calls=%fused_computation.4 | convolution fusion | flops 50331712 | bytes 5242944 | tf_op jit(solution)/shard_map/dpsq,sr->dprq/dot_general | solution.py:48
  11.0 1.1 convolution_bitcast_fusion
  12.3 2.5 %fusion = f32[3,32,4,128]{3,0,2,1:T(4,128)S(1)} fusion(f32[32,32,4,128]{3,1,2,0:T(8,128)S(1)} %convolution_bitcast_fusion, s32[32]{0:T(128)S(1)} %dynamic_slice.8, s32[3]{0:T(128)S(1)} %iota_add_fusion), kind=kOutput, calls=%fused_computation.1 | convolution fusion | flops 18874464 | bytes 2293900 | tf_op jit(solution)/shard_map/dcrq,dk->kcrq/dot_general | solution.py:59
  14.8 1.3 collective-permute-start.1
  16.1 3.0 %collective-permute-start = (f32[1,32,4,128]{3,0,2,1:T(1,128)S(1)}, f32[1,32,4,128]{3,0,2,1:T(1,128)S(1)}, u32[]{:S(2)}, u32[]{:S(2)}) collective-permute-start(f32[1,32,4,128]{3,0,2,1:T(1,128)S(1)} %get-tuple-element.58), channel_id=1, source_target_pairs={{0,1},{1,2},{2,3},{3,4},{4,5},{5,6},{6,7},{7,8},{8,9},{9,10},{10,1... | collective-permute-start | bytes 196616 | tf_op jit(solution)/shard_map/ppermute | solution.py:16
  19.2 0.6 gather_fusion
  19.9 1.3 fusion.8
  21.2 0.1 convert_reduce_fusion.2
  21.4 0.1 convert_reduce_fusion
  21.5 0.2 multiply_sqrt_fusion
  21.7 0.6 dynamic_slice.9
  22.9 0.7 maximum_sqrt_fusion.5
  24.7 0.1 copy.34
  24.9 0.2 fusion.25
  25.1 0.8 broadcast_divide_fusion.2
  26.0 0.7 bitcast_divide_fusion
  26.6 0.7 bitcast_divide_fusion.1
  27.3 0.5 divide_bitcast_fusion
  27.8 124.4 %all-reduce.2.cloned.1.call-done = f32[4,32,4,128]{3,0,2,1:T(4,128)} async-done(((f32[4,32,4,128]{3,0,2,1:T(4,128)}), f32[4,32,4,128]{3,0,2,1:T(4,128)}) %all-reduce.2.cloned.1.call-update) | async-done | bytes 262160 | tf_op jit(solution)/shard_map/psum | solution.py:67
  152.2 1.2 fusion.24
  153.4 0.8 copy.37
  154.2 0.6 copy.38
  154.9 0.6 copy.39
  155.6 0.7 broadcast_divide_fusion.4
  (28 shorter events, 1.0 us)
Async XLA Ops:
  7.2 145.0 %all-reduce.2.cloned.1.call-start = ((), (), s32[]{:S(2)}) async-start(), calls=%async_computation | async-start | bytes 524288 | tf_op jit(solution)/shard_map/psum | solution.py:67
  7.2 3.8 %copy-start.2 = (s32[16]{0:T(128)S(1)}, s32[16]{0:T(128)}, u32[]{:S(2)}) copy-start(s32[16]{0:T(128)} %param.8) | copy-start | bytes 196
  11.0 1.2 copy-start.1
  12.1 7.1 %copy-start = (s32[32]{0:T(128)S(1)}, s32[32]{0:T(128)}, u32[]{:S(2)}) copy-start(s32[32]{0:T(128)} %param.7) | copy-start | bytes 388
  12.2 9.0 %copy-start.3 = (s32[16]{0:T(128)S(1)}, s32[16]{0:T(128)}, u32[]{:S(2)}) copy-start(s32[16]{0:T(128)} %param.9) | copy-start | bytes 196
  14.8 10.1 %collective-permute-start.1 = (f32[1,32,4,128]{3,0,2,1:T(1,128)S(1)}, f32[1,32,4,128]{3,0,2,1:T(1,128)S(1)}, u32[]{:S(2)}, u32[]{:S(2)}) collective-permute-start(f32[1,32,4,128]{3,0,2,1:T(1,128)S(1)} %get-tuple-element.59), channel_id=1, source_target_pairs={{1,0},{2,1},{3,2},{4,3},{5,4},{6,5},{7,6},{8,7},{9,8},{10,9},{11,1... | collective-permute-start | bytes 196616 | tf_op jit(solution)/shard_map/ppermute | solution.py:19
  16.1 8.8 %collective-permute-start = (f32[1,32,4,128]{3,0,2,1:T(1,128)S(1)}, f32[1,32,4,128]{3,0,2,1:T(1,128)S(1)}, u32[]{:S(2)}, u32[]{:S(2)}) collective-permute-start(f32[1,32,4,128]{3,0,2,1:T(1,128)S(1)} %get-tuple-element.58), channel_id=1, source_target_pairs={{0,1},{1,2},{2,3},{3,4},{4,5},{5,6},{6,7},{7,8},{8,9},{9,10},{10,1... | collective-permute-start | bytes 196616 | tf_op jit(solution)/shard_map/ppermute | solution.py:16
Sparse Core Ops, SparseCore 0:
  21.3 130.8 all-reduce.1
where the time goes:
time: 163 us
  waiting for transfers between devices  124 us (76%)
  between operations  15.6 us (10%)
  matrix products  8.79 us (5%)
  other arithmetic  6.2 us (4%)
  starting transfers between devices  4.36 us (3%)
  local copies, waits for them, and re-layouts  3.75 us (2%)
    psum x1, waiting for transfers between devices, shards(): year_cube = lax.psum(year_part, ('tm', 'prod'))  124 us
    dot_general x1, matrix products, shards(): jnp.einsum('dpsq,sr->dprq', sales_records, region_hot, precision=highest)  3.76 us
    div x7, other arithmetic, scaled(): return sums / jnp.sqrt(counts)  3.52 us
  transfers between devices with their start and end apart: 3, of which 1 were waited for; matrix products, arithmetic and copies ran while one was open for 4% of the time, Pallas kernels for 0%

commit v1 on v0

--- a/solution.py
+++ b/solution.py
@@ -30,6 +30,10 @@
 
 
 def shards(sales_records, day_month, month_year, product_category, store_region):
+
+    def lead_core_by_axis(here_x):
+        return jnp.sum(jax.lax.all_gather(here_x, ("tm", "prod")), 0)
+
     highest = lax.Precision.HIGHEST
     day_dev = sales_records.shape[0]
     prod_dev = sales_records.shape[1]
@@ -64,7 +68,7 @@
     summed = padded[0:1] + padded[2:3] + padded[4:5]
     detail = lax.psum_scatter(summed, "prod", scatter_dimension=1, tiled=True)
     year_part = jnp.einsum("mcrq,my->ycrq", partial_value, source_years, precision=highest)
-    year_cube = lax.psum(year_part, ("tm", "prod"))
+    year_cube = lead_core_by_axis(year_part)
     cell = own_days[:, None, None] * own_sizes[None, :, None] * region_size[None, None, :]
     month_detail = scaled(detail, jnp.maximum(cell, 1.0)[..., None])
     month_cat = jnp.sum(detail, 2)

time: 163 us -> 117 us (0.72)
  waiting for transfers between devices: 124 us -> 69.5 us
  other arithmetic: 6.2 us -> 14.8 us
    psum x1 -> x0, waiting for transfers between devices: 124 us -> none  [shards(): year_cube = lax.psum(year_part, ('tm', 'prod'))]
    all_gather x0 -> x1, waiting for transfers between devices: none -> 69.3 us  [lead_core_by_axis(): return jnp.sum(jax.lax.all_gather(here_x, ('tm', 'prod')), 0)]
    reduce_sum x0 -> x1, other arithmetic: none -> 4.26 us  [lead_core_by_axis(): return jnp.sum(jax.lax.all_gather(here_x, ('tm', 'prod')), 0)]
    reduce_sum x1 -> x2, other arithmetic: 1.18 us -> 5.04 us  [shards(): jnp.sum(year_reg, 1)]
    div x7 -> x8, other arithmetic: 3.52 us -> 3.77 us  [scaled(): return sums / jnp.sqrt(counts)]
  transfers between devices with their start and end apart: 3 -> 3, of which waited for: 1 -> 2; matrix products, arithmetic and copies ran while one was open for 4% -> 5% of each run, Pallas kernels for 0% -> 0%
where the time goes in v1:
time: 117 us
  waiting for transfers between devices  69.5 us (59%)
  between operations  15.6 us (13%)
  other arithmetic  14.8 us (13%)
  matrix products  8.1 us (7%)
  local copies, waits for them, and re-layouts  5.2 us (4%)
  starting transfers between devices  3.73 us (3%)
    all_gather x1, waiting for transfers between devices, lead_core_by_axis(): return jnp.sum(jax.lax.all_gather(here_x, ('tm', 'prod')), 0)  69.3 us
    reduce_sum x2, other arithmetic, shards(): jnp.sum(year_reg, 1)  5.04 us
    reduce_sum x1, other arithmetic, lead_core_by_axis(): return jnp.sum(jax.lax.all_gather(here_x, ('tm', 'prod')), 0)  4.26 us
    div x8, other arithmetic, scaled(): return sums / jnp.sqrt(counts)  3.77 us
    dot_general x1, matrix products, shards(): jnp.einsum('dpsq,sr->dprq', sales_records, region_hot, precision=highest)  3.76 us
    dot_general x1, matrix products, shards(): jnp.einsum('dcrq,dk->kcrq', by_category, window_hot, precision=highest)  2.46 us
    ppermute x1, starting transfers between devices, with_halo(): lax.ppermute(lax.slice_in_dim(block, block.shape[dim] - width, None, axis...  2.4 us
  transfers between devices with their start and end apart: 3, of which 2 were waited for; matrix products, arithmetic and copies ran while one was open for 5% of the time, Pallas kernels for 0%

profile of v1, /device:TPU:0, one launch (start us, length us, event | category | flops | bytes accessed | tf_op | source)
XLA Modules:
  0.0 116.8 jit_solution(17558224526090363138)
XLA Ops:
  7.3 0.8 dynamic_slice.8
  8.0 3.8 %convolution_bitcast_fusion.1 = f32[32,16,4,128]{3,2,1,0:T(4,128)S(1)} fusion(f32[32,16,16,128]{3,2,1,0:T(8,128)} %param.5, s32[16]{0:T(128)} %param.9), kind=kOutput, calls=%fused_computation.4 | convolution fusion | flops 50331712 | bytes 5242944 | tf_op jit(solution)/shard_map/dpsq,sr->dprq/dot_general | solution.py:52
  11.8 1.1 convolution_bitcast_fusion
  13.0 0.6 gather_fusion
  13.6 2.5 %fusion = f32[3,32,4,128]{3,0,2,1:T(4,128)S(1)} fusion(f32[32,32,4,128]{3,1,2,0:T(8,128)S(1)} %convolution_bitcast_fusion, s32[32]{0:T(128)S(1)} %dynamic_slice.8, s32[3]{0:T(128)S(1)} %iota_add_fusion), kind=kOutput, calls=%fused_computation.1 | convolution fusion | flops 18874464 | bytes 2293900 | tf_op jit(solution)/shard_map/dcrq,dk->kcrq/dot_general | solution.py:63
  16.1 0.6 fusion.8
  16.6 0.8 copy.58
  17.6 2.4 %collective-permute-start = (f32[1,32,4,128]{3,0,2,1:T(1,128)S(1)}, f32[1,32,4,128]{3,0,2,1:T(1,128)S(1)}, u32[]{:S(2)}, u32[]{:S(2)}) collective-permute-start(f32[1,32,4,128]{3,0,2,1:T(1,128)S(1)} %get-tuple-element.73), channel_id=1, source_target_pairs={{0,1},{1,2},{2,3},{3,4},{4,5},{5,6},{6,7},{7,8},{8,9},{9,10},{10,1... | collective-permute-start | bytes 196616 | tf_op jit(solution)/shard_map/ppermute | solution.py:16
  20.0 1.3 %collective-permute-start.1 = (f32[1,32,4,128]{3,0,2,1:T(1,128)S(1)}, f32[1,32,4,128]{3,0,2,1:T(1,128)S(1)}, u32[]{:S(2)}, u32[]{:S(2)}) collective-permute-start(f32[1,32,4,128]{3,0,2,1:T(1,128)S(1)} %get-tuple-element.74), channel_id=1, source_target_pairs={{1,0},{2,1},{3,2},{4,3},{5,4},{6,5},{7,6},{8,7},{9,8},{10,9},{11,1... | collective-permute-start | bytes 196616 | tf_op jit(solution)/shard_map/ppermute | solution.py:19
  21.4 0.6 dynamic_slice.9
  22.9 0.7 maximum_sqrt_fusion.5
  23.5 0.2 multiply_sqrt_fusion
  25.4 0.5 divide_bitcast_fusion
  25.9 0.7 bitcast_divide_fusion.1
  26.6 0.7 bitcast_divide_fusion
  27.2 0.8 broadcast_divide_fusion
  28.1 69.3 %all-gather.3.cloned.1.call-done = f32[128,32,4,128]{3,1,2,0:T(8,128)} async-done(((f32[4,32,4,128]{3,1,2,0:T(8,128)}), f32[128,32,4,128]{3,1,2,0:T(8,128)}) %all-gather.3.cloned.1.call-update) | async-done | bytes 8388624 | tf_op jit(solution)/shard_map/all_gather | solution.py:35
  97.4 5.0 %fusion.24 = (f32[128,128]{1,0:T(8,128)S(1)}, f32[128,32,128]{2,1,0:T(8,128)S(1)}, f32[128,4,128]{2,1,0:T(4,128)S(1)}) fusion(f32[128,32,4,128]{3,1,2,0:T(8,128)} %all-gather.3.cloned.1.call-done), kind=kLoop, calls=%fused_computation.57 | loop fusion | flops 5685248 | bytes 10813440 | tf_op jit(solution)/shard_map/reduce_sum | solution.py:93
  102.5 0.6 copy.68
  103.1 4.3 %reduce_sum.102 = f32[4,32,4,128]{3,1,2,0:T(8,128)S(1)} reduce(f32[32,4,32,4,128]{4,2,3,1,0:T(8,128)} %bitcast.53, f32[]{:T(128)} %constant.17.clone.1), dimensions={0}, to_apply=%region_6.7 | reduce | flops 2031616 | bytes 8650756 | tf_op jit(solution)/shard_map/reduce_sum | solution.py:35
  107.4 0.2 copy_divide_fusion
  107.6 0.8 copy.66
  108.7 0.6 copy.67
  109.3 0.7 broadcast_divide_fusion.1
  (34 shorter events, 1.9 us)
Async XLA Ops:
  7.2 90.2 %all-gather.3.cloned.1.call-start = ((), (), s32[]{:S(2)}) async-start(), calls=%async_computation | async-start | bytes 8650752 | tf_op jit(solution)/shard_map/all_gather | solution.py:35
  8.0 3.8 %copy-start.2 = (s32[16]{0:T(128)S(1)}, s32[16]{0:T(128)}, u32[]{:S(2)}) copy-start(s32[16]{0:T(128)} %param.8) | copy-start | bytes 196
  11.8 1.1 copy-start
  13.6 7.7 %copy-start.1 = (s32[1024]{0:T(1024)S(1)}, s32[1024]{0:T(1024)}, u32[]{:S(2)}) copy-start(s32[1024]{0:T(1024)} %param.6) | copy-start | bytes 12292
  13.6 9.0 %copy-start.3 = (s32[16]{0:T(128)S(1)}, s32[16]{0:T(128)}, u32[]{:S(2)}) copy-start(s32[16]{0:T(128)} %param.9) | copy-start | bytes 196
  17.6 7.5 %collective-permute-start = (f32[1,32,4,128]{3,0,2,1:T(1,128)S(1)}, f32[1,32,4,128]{3,0,2,1:T(1,128)S(1)}, u32[]{:S(2)}, u32[]{:S(2)}) collective-permute-start(f32[1,32,4,128]{3,0,2,1:T(1,128)S(1)} %get-tuple-element.73), channel_id=1, source_target_pairs={{0,1},{1,2},{2,3},{3,4},{4,5},{5,6},{6,7},{7,8},{8,9},{9,10},{10,1... | collective-permute-start | bytes 196616 | tf_op jit(solution)/shard_map/ppermute | solution.py:16
  20.0 5.2 %collective-permute-start.1 = (f32[1,32,4,128]{3,0,2,1:T(1,128)S(1)}, f32[1,32,4,128]{3,0,2,1:T(1,128)S(1)}, u32[]{:S(2)}, u32[]{:S(2)}) collective-permute-start(f32[1,32,4,128]{3,0,2,1:T(1,128)S(1)} %get-tuple-element.74), channel_id=1, source_target_pairs={{1,0},{2,1},{3,2},{4,3},{5,4},{6,5},{7,6},{8,7},{9,8},{10,9},{11,1... | collective-permute-start | bytes 196616 | tf_op jit(solution)/shard_map/ppermute | solution.py:19
Sparse Core Ops, SparseCore 0:
  17.6 79.7 all-gather.2
